TPU v7x, 128 devices: a whole 4x4x4 slice. The times are simulated.
128 devices in a mesh: dp: 16 (over y, x), mp: 8 (over z, core).
Axes of the slice: x: 4, y: 4, z: 4, core: 2. Of those that a mesh axis runs over, the one named last changes fastest.
Arguments:
- tokens: bfloat16 [65536, 1024], P(('dp', 'mp')), may hold values from -6 to 6
- norm_gain: float32 [2, 1024], replicated, may hold values from 0.1 to 1.9
- qkv_weight: bfloat16 [3, 1024, 1024], P(None, 'dp', 'mp')
- out_weight: bfloat16 [1024, 1024], P('mp', 'dp'), may hold values from -0.1875 to 0.1875
- variate_bias: float32 [2, 16], replicated, may hold values from -6 to 6
- ffn_weight: bfloat16 [2, 1024, 2816], P(None, 'dp', 'mp'), may hold values from -0.1875 to 0.1875
- down_weight: bfloat16 [2816, 1024], P('mp', 'dp'), may hold values from -0.109375 to 0.109375
- sample_ids: int32 [65536], P(('dp', 'mp')), may hold values from 0 to 127, as said below
- variate_ids: int32 [65536], P(('dp', 'mp')), may hold values from 0 to 15, as said below
- time_ids: int32 [65536], P(('dp', 'mp')), may hold values from 0 to 31, as said below
Outputs:
- encoded: bfloat16 [65536, 1024], P(('dp', 'mp'))
Inputs may be any that keep to these rules, and one draw needn't show every extreme that they name: `sample_ids`: within each packed sequence of 512 tokens the series numbers start at 0 and never fall; a series with v variates (1 to 16) and p patches (4 to 32) holds v * p consecutive tokens, the last series of a sequence may be cut short; some packed sequence holds 128 series of one variate and four patches each. `variate_ids`: A token's offset within its series divided by that series' patch count p. `time_ids`: A token's offset within its series modulo that series' patch count p.
All inputs are finite; a program needn't handle non-finite values.
Results may differ from a plain program's by a relative error of at most 0.017.
Values may be sent and summed in bfloat16 or wider, within the bound.
A program may use at most 128 MiB of HBM per device.

v0:
```python
import jax
import jax.numpy as jnp
from jax import lax
from jax.sharding import PartitionSpec as P

HEAD_DIM = 64
L = 512


def sent_to_all(shard, axis):
    copies = jnp.broadcast_to(shard, (lax.axis_size(axis), *shard.shape))
    return lax.all_to_all(copies, axis, split_axis=0, concat_axis=0, tiled=True)


def in_order(blocks, dim):
    blocks = jnp.moveaxis(blocks, 0, dim)
    dims = blocks.shape
    return blocks.reshape(*dims[:dim], dims[dim] * dims[dim + 1], *dims[dim + 2 :])


def collect(shard, axis, dim):
    blocks = sent_to_all(shard, axis)
    return in_order(blocks, dim)


def rows_first(arrays, axis, dims):
    turned = [jnp.moveaxis(a, dim, 0) for a, dim in zip(arrays, dims)]
    widths = [t[0].size for t in turned]
    both = jnp.concatenate([t.reshape(-1, w) for t, w in zip(turned, widths)], axis=1)
    whole = lax.all_gather(both, axis, axis=0, tiled=True)
    blocks = jnp.split(whole, [sum(widths[:k]) for k in range(1, len(widths))], axis=1)
    return tuple(
        (
            jnp.moveaxis(b.reshape(-1, *t.shape[1:]), 0, dim)
            for b, t, dim in zip(blocks, turned, dims)
        )
    )


def rms_norm(values, gain):
    wide = values.astype(jnp.float32)
    square = jnp.mean(wide * wide, axis=-1, keepdims=True)
    return (wide * lax.rsqrt(square + 1e-05) * gain[None, :]).astype(jnp.bfloat16)


def rotate(values, times):
    half = values.shape[-1] // 2
    freq = 10000.0 ** (-jnp.arange(half, dtype=jnp.float32) / half)
    angle = times.astype(jnp.float32)[:, None] * freq[None, :]
    cosine = jnp.cos(angle)[:, None, :]
    sine = jnp.sin(angle)[:, None, :]
    first = values[..., :half]
    second = values[..., half:]
    return jnp.concatenate(
        [first * cosine - second * sine, first * sine + second * cosine], axis=-1
    )


def rotated(raw, times):
    row_total, local_width = raw.shape
    turned = rotate(raw.reshape(row_total, local_width // HEAD_DIM, HEAD_DIM), times)
    return turned.reshape(row_total, local_width).astype(jnp.bfloat16)


def attend(queries, keys_rot, values, samples, variates, bias):
    row_total, local_width = queries.shape
    heads_here = local_width // HEAD_DIM
    count = row_total // L

    def one_sequence(args):
        qs, ks, vs, sample_row, variate_row = args
        scores = jnp.einsum(
            "qhd,khd->hqk", qs, ks, preferred_element_type=jnp.float32
        ) * HEAD_DIM ** (-0.5)
        same = variate_row[:, None] == variate_row[None, :]
        scores = scores + jnp.where(same[None], bias[0][:, None, None], bias[1][:, None, None])
        scores = jnp.where((sample_row[:, None] == sample_row[None, :])[None], scores, -1e30)
        top = jnp.max(scores, axis=2, keepdims=True)
        expo = jnp.exp(scores - top)
        weights = (expo / jnp.sum(expo, axis=2, keepdims=True)).astype(jnp.bfloat16)
        return jnp.einsum("hqk,khd->qhd", weights, vs, preferred_element_type=jnp.float32).astype(
            jnp.bfloat16
        )

    shape = (count, L, heads_here, HEAD_DIM)
    result = lax.map(
        one_sequence,
        (
            queries.reshape(shape),
            keys_rot.reshape(shape),
            values.reshape(shape),
            samples.reshape(count, L),
            variates.reshape(count, L),
        ),
    )
    return result.reshape(row_total, local_width)


def local(
    tokens,
    norm_gain,
    qkv_weight,
    out_weight,
    variate_bias,
    ffn_weight,
    down_weight,
    sample_ids,
    variate_ids,
    time_ids,
):
    heads_here = qkv_weight.shape[2] // HEAD_DIM
    head_start = lax.axis_index("mp") * heads_here
    bias_local = lax.dynamic_slice_in_dim(variate_bias, head_start, heads_here, 1)
    first_normed = rms_norm(tokens, norm_gain[0])
    wide_columns = collect(qkv_weight, "mp", 2)
    columns = first_normed
    projected = jnp.einsum(
        "rc,jcd->jrd",
        columns,
        lax.all_gather(wide_columns, "dp", axis=1, tiled=True),
        preferred_element_type=jnp.float32,
    )
    queries = rotated(projected[0], time_ids)
    keys_rot = rotated(projected[1], time_ids)
    values = projected[2].astype(jnp.bfloat16)
    grouped = lax.all_to_all(
        jnp.stack([queries, keys_rot, values]), "mp", split_axis=2, concat_axis=1, tiled=True
    )
    gathered_ids = rows_first((sample_ids, variate_ids), "mp", (0, 0))
    attended = attend(
        grouped[0], grouped[1], grouped[2], gathered_ids[0], gathered_ids[1], bias_local
    )
    back_rows = lax.all_to_all(attended, "mp", split_axis=0, concat_axis=1, tiled=True)
    out_rows = collect(out_weight, "mp", 0)
    mixed = jnp.dot(back_rows, collect(out_rows, "dp", 1), preferred_element_type=jnp.float32)
    residual = (tokens.astype(jnp.float32) + mixed).astype(jnp.bfloat16)
    second_normed = rms_norm(residual, norm_gain[1])
    ffn_columns = collect(ffn_weight, "mp", 2)
    columns = second_normed
    gate_up = jnp.einsum(
        "rc,jcf->jrf",
        columns,
        lax.all_gather(ffn_columns, "dp", axis=1, tiled=True),
        preferred_element_type=jnp.float32,
    )
    hidden = (jax.nn.silu(gate_up[0]) * gate_up[1]).astype(jnp.bfloat16)
    down_full = collect(down_weight, "mp", 0)
    feed = jnp.dot(
        hidden,
        lax.all_gather(down_full, "dp", axis=1, tiled=True),
        preferred_element_type=jnp.float32,
    )
    return (residual.astype(jnp.float32) + feed).astype(jnp.bfloat16)


def solution(mesh):
    return jax.shard_map(
        local,
        mesh=mesh,
        in_specs=(
            P(("dp", "mp"), None),
            P(),
            P(None, "dp", "mp"),
            P("mp", "dp"),
            P(),
            P(None, "dp", "mp"),
            P("mp", "dp"),
            P(("dp", "mp")),
            P(("dp", "mp")),
            P(("dp", "mp")),
        ),
        out_specs=P(("dp", "mp"), None),
        check_vma=False,
    )
```

profile of v0, /device:TPU:2, one launch (start us, length us, event | category | flops | bytes accessed | tf_op | source)
XLA Modules:
  0.0 293.8 jit_solution(12576738158072073453)
XLA Ops:
  7.5 14.0 %all_to_all.59 = bf16[8,3,64,128]{3,2,1,0:T(8,128)(2,1)S(1)} all-to-all(bf16[8,3,64,128]{3,2,1,0:T(8,128)(2,1)S(1)} %broadcast_in_dim.81), channel_id=1, replica_groups=mesh['dp'=16,'mp'=8] {'mp'}, dimensions={0} | all-to-all | bytes 786432 | tf_op jit(solution)/shard_map/all_to_all | solution.py:12
  22.5 15.6 %all_to_all.60 = bf16[8,2,64,352]{3,2,1,0:T(8,128)(2,1)S(1)} all-to-all(bf16[8,2,64,352]{3,2,1,0:T(8,128)(2,1)S(1)} %broadcast_in_dim.84), channel_id=1, replica_groups=mesh['dp'=16,'mp'=8] {'mp'}, dimensions={0} | all-to-all | bytes 1441792 | tf_op jit(solution)/shard_map/all_to_all | solution.py:12
  40.8 3.4 %all-to-all-start.3 = ((bf16[8,128,64]{1,2,0:T(8,128)(2,1)}), bf16[8,128,64]{1,2,0:T(8,128)(2,1)S(1)}, u32[]{:S(2)}, u32[]{:S(2)}) async-start(bf16[8,128,64]{1,2,0:T(8,128)(2,1)} %broadcast_in_dim.82), calls=%async_computation.3 | async-start | bytes 262144 | tf_op jit(solution)/shard_map/all_to_all | solution.py:12
  44.9 38.3 %all-gather.4.cloned.1.call-done = bf16[3,1024,1024]{2,1,0:T(8,128)(2,1)} async-done(((bf16[3,64,1024]{2,1,0:T(8,128)(2,1)}), bf16[3,1024,1024]{2,1,0:T(8,128)(2,1)}) %all-gather.4.cloned.1.call-update) | async-done | bytes 6291472 | tf_op jit(solution)/shard_map/all_gather | solution.py:120
  83.1 5.7 %convolution_bitcast_fusion.1 = f32[3,512,1024]{2,1,0:T(8,128)S(1)} fusion(bf16[3,1024,1024]{2,1,0:T(8,128)(2,1)} %all-gather.4.cloned.1.call-done, bf16[512,1024]{1,0:T(8,128)(2,1)S(1)} %copy-done.4, f32[1024]{0:T(1024)S(1)} %bitcast.142, f32[512]{0:T(512)S(1)} %add_rsqrt_fusion.1), kind=kOutput, calls=%fused_computation.45 | convolution fusion | flops 3223322624 | bytes 13637632 | tf_op jit(solution)/shard_map/rc,jcd->jrd/dot_general | solution.py:117
  88.9 2.5 fusion.69
  94.6 3.1 %copy.37 = f32[1,512,1024]{1,2,0:T(8,128)} copy(f32[1,512,1024]{2,1,0:T(8,128)} %get-tuple-element.71) | data formatting | bytes 4194304 | tf_op jit(solution)/shard_map/slice | solution.py:124
  97.7 3.3 %subtract_convert_fusion.1 = (bf16[512,16,32]{0,2,1:T(8,128)(2,1)S(1)}, bf16[512,16,32]{0,2,1:T(8,128)(2,1)S(1)}, bf16[512,16,32]{0,2,1:T(8,128)(2,1)}, bf16[512,16,32]{0,2,1:T(8,128)(2,1)}) fusion(f32[512,16,64]{0,2,1:T(8,128)S(1)} %bitcast.128, f32[512,32]{0,1:T(8,128)S(1)} %get-tuple-element.84, f32[512,32]{0,1:T(8,128)S(1)} %get-tuple-element.83, ...), kind=kLoop, calls=%fused_computation.64 | loop fusion | flops 4194304 | bytes 6422528 | tf_op jit(solution)/shard_map/convert.3
  101.0 2.8 slice.103
  104.6 4.4 %all-to-all-start.6 = ((bf16[8,352,64]{1,2,0:T(8,128)(2,1)}), bf16[8,352,64]{1,2,0:T(8,128)(2,1)S(1)}, u32[]{:S(2)}, u32[]{:S(2)}) async-start(bf16[8,352,64]{1,2,0:T(8,128)(2,1)} %broadcast_in_dim.85), calls=%async_computation.6 | async-start | bytes 786432 | tf_op jit(solution)/shard_map/all_to_all | solution.py:12
  115.5 5.7 %copy.40 = bf16[3,512,1024]{1,0,2:T(4,128)(2,1)} copy(bf16[3,512,1024]{2,1,0:T(8,128)(2,1)S(1)} %pad_maximum_fusion) | data formatting | bytes 6291456 | tf_op jit(solution)/shard_map/stack | solution.py:127
  121.2 4.9 %all-to-all-start.1 = ((bf16[3,512,1024]{1,0,2:T(4,128)(2,1)}), bf16[3,512,1024]{1,0,2:T(4,128)(2,1)}, u32[]{:S(2)}, u32[]{:S(2)}) async-start(bf16[3,512,1024]{1,0,2:T(4,128)(2,1)} %copy.40), calls=%async_computation.1 | async-start | bytes 8388608 | tf_op jit(solution)/shard_map/all_to_all | solution.py:126
  126.2 55.5 %all_gather.13 = s32[4096,2]{0,1:T(2,128)S(1)} all-gather(s32[512,2]{0,1:T(2,128)S(1)} %pad_add_fusion), channel_id=1, replica_groups=mesh['dp'=16,'mp'=8] {'mp'}, dimensions={0}, use_global_device_ids=true | all-gather | bytes 36864 | tf_op jit(solution)/shard_map/all_gather | solution.py:30
  184.9 5.8 %all-to-all-start.4 = ((bf16[16,1024,64]{1,2,0:T(8,128)(2,1)}), bf16[16,1024,64]{1,2,0:T(8,128)(2,1)S(1)}, u32[]{:S(2)}, u32[]{:S(2)}) async-start(bf16[16,1024,64]{1,2,0:T(8,128)(2,1)} %broadcast_in_dim.83), calls=%async_computation.4 | async-start | bytes 4194304 | tf_op jit(solution)/shard_map/all_to_all | solution.py:12
  190.7 3.2 %copy.41 = bf16[3,512,1024]{1,2,0:T(8,128)(2,1)S(1)} copy(bf16[3,512,1024]{1,0,2:T(4,128)(2,1)} %all-to-all-done.1) | data formatting | bytes 6291456 | tf_op jit(solution)/shard_map/all_to_all | solution.py:126
  195.7 47.5 %while.10 = (s32[]{:T(128)}, bf16[8,512,2,64]{1,3,2,0:T(8,128)(2,1)}, bf16[8,512,2,64]{1,3,2,0:T(8,128)(2,1)}, s32[8,512]{1,0:T(8,128)S(1)}, bf16[8,512,2,64]{1,...) while((s32[]{:T(128)}, ...), condition=%wide.region_4.5_spmd, body=%wide.region_1.4_spmd.sunk | while | flops 208734208 | bytes 2383009 | solution.py:86
  198.4 3.2 %fusion.92 = bf16[8,512,2,64]{1,3,2,0:T(8,128)(2,1)} fusion(bf16[8,512,2,64]{1,3,2,0:T(8,128)(2,1)} %get-tuple-element.156, s32[]{:T(128)} %get-tuple-element.155, f32[2,512]{1,0:T(2,128)S(1)} %fusion.91, bf16[8,512,2,64]{1,3,2,0:T(8,128)(2,1)} %get-tuple-element.166, f32[2]{0:T(128)S(1)} %get-tuple-element.142, f32[2]{0:T(128)S(1)} %get-tuple-element.143, ...), kind=kOutput, calls=%fused_computation.6.clone.1 | convolution fusion | flops 137954816 | bytes 1054736 | tf_op jit(solution)/shard_map/while/body/eval_jaxpr/hqk,khd->qhd/dot_general | solution.py:81
  202.1 2.2 fusion.91
  204.3 3.2 %fusion.92 = bf16[8,512,2,64]{1,3,2,0:T(8,128)(2,1)} fusion(bf16[8,512,2,64]{1,3,2,0:T(8,128)(2,1)} %get-tuple-element.156, s32[]{:T(128)} %get-tuple-element.155, f32[2,512]{1,0:T(2,128)S(1)} %fusion.91, bf16[8,512,2,64]{1,3,2,0:T(8,128)(2,1)} %get-tuple-element.166, f32[2]{0:T(128)S(1)} %get-tuple-element.142, f32[2]{0:T(128)S(1)} %get-tuple-element.143, ...), kind=kOutput, calls=%fused_computation.6.clone.1 | convolution fusion | flops 137954816 | bytes 1054736 | tf_op jit(solution)/shard_map/while/body/eval_jaxpr/hqk,khd->qhd/dot_general | solution.py:81
  208.0 2.2 fusion.91
  210.2 3.2 %fusion.92 = bf16[8,512,2,64]{1,3,2,0:T(8,128)(2,1)} fusion(bf16[8,512,2,64]{1,3,2,0:T(8,128)(2,1)} %get-tuple-element.156, s32[]{:T(128)} %get-tuple-element.155, f32[2,512]{1,0:T(2,128)S(1)} %fusion.91, bf16[8,512,2,64]{1,3,2,0:T(8,128)(2,1)} %get-tuple-element.166, f32[2]{0:T(128)S(1)} %get-tuple-element.142, f32[2]{0:T(128)S(1)} %get-tuple-element.143, ...), kind=kOutput, calls=%fused_computation.6.clone.1 | convolution fusion | flops 137954816 | bytes 1054736 | tf_op jit(solution)/shard_map/while/body/eval_jaxpr/hqk,khd->qhd/dot_general | solution.py:81
  216.1 3.2 %fusion.92 = bf16[8,512,2,64]{1,3,2,0:T(8,128)(2,1)} fusion(bf16[8,512,2,64]{1,3,2,0:T(8,128)(2,1)} %get-tuple-element.156, s32[]{:T(128)} %get-tuple-element.155, f32[2,512]{1,0:T(2,128)S(1)} %fusion.91, bf16[8,512,2,64]{1,3,2,0:T(8,128)(2,1)} %get-tuple-element.166, f32[2]{0:T(128)S(1)} %get-tuple-element.142, f32[2]{0:T(128)S(1)} %get-tuple-element.143, ...), kind=kOutput, calls=%fused_computation.6.clone.1 | convolution fusion | flops 137954816 | bytes 1054736 | tf_op jit(solution)/shard_map/while/body/eval_jaxpr/hqk,khd->qhd/dot_general | solution.py:81
  222.0 3.2 %fusion.92 = bf16[8,512,2,64]{1,3,2,0:T(8,128)(2,1)} fusion(bf16[8,512,2,64]{1,3,2,0:T(8,128)(2,1)} %get-tuple-element.156, s32[]{:T(128)} %get-tuple-element.155, f32[2,512]{1,0:T(2,128)S(1)} %fusion.91, bf16[8,512,2,64]{1,3,2,0:T(8,128)(2,1)} %get-tuple-element.166, f32[2]{0:T(128)S(1)} %get-tuple-element.142, f32[2]{0:T(128)S(1)} %get-tuple-element.143, ...), kind=kOutput, calls=%fused_computation.6.clone.1 | convolution fusion | flops 137954816 | bytes 1054736 | tf_op jit(solution)/shard_map/while/body/eval_jaxpr/hqk,khd->qhd/dot_general | solution.py:81
  228.0 3.2 %fusion.92 = bf16[8,512,2,64]{1,3,2,0:T(8,128)(2,1)} fusion(bf16[8,512,2,64]{1,3,2,0:T(8,128)(2,1)} %get-tuple-element.156, s32[]{:T(128)} %get-tuple-element.155, f32[2,512]{1,0:T(2,128)S(1)} %fusion.91, bf16[8,512,2,64]{1,3,2,0:T(8,128)(2,1)} %get-tuple-element.166, f32[2]{0:T(128)S(1)} %get-tuple-element.142, f32[2]{0:T(128)S(1)} %get-tuple-element.143, ...), kind=kOutput, calls=%fused_computation.6.clone.1 | convolution fusion | flops 137954816 | bytes 1054736 | tf_op jit(solution)/shard_map/while/body/eval_jaxpr/hqk,khd->qhd/dot_general | solution.py:81
  231.6 2.4 fusion.91
  234.0 3.2 %fusion.92 = bf16[8,512,2,64]{1,3,2,0:T(8,128)(2,1)} fusion(bf16[8,512,2,64]{1,3,2,0:T(8,128)(2,1)} %get-tuple-element.156, s32[]{:T(128)} %get-tuple-element.155, f32[2,512]{1,0:T(2,128)S(1)} %fusion.91, bf16[8,512,2,64]{1,3,2,0:T(8,128)(2,1)} %get-tuple-element.166, f32[2]{0:T(128)S(1)} %get-tuple-element.142, f32[2]{0:T(128)S(1)} %get-tuple-element.143, ...), kind=kOutput, calls=%fused_computation.6.clone.1 | convolution fusion | flops 137954816 | bytes 1054736 | tf_op jit(solution)/shard_map/while/body/eval_jaxpr/hqk,khd->qhd/dot_general | solution.py:81
  237.7 2.2 fusion.91
  239.9 3.2 %fusion.92 = bf16[8,512,2,64]{1,3,2,0:T(8,128)(2,1)} fusion(bf16[8,512,2,64]{1,3,2,0:T(8,128)(2,1)} %get-tuple-element.156, s32[]{:T(128)} %get-tuple-element.155, f32[2,512]{1,0:T(2,128)S(1)} %fusion.91, bf16[8,512,2,64]{1,3,2,0:T(8,128)(2,1)} %get-tuple-element.166, f32[2]{0:T(128)S(1)} %get-tuple-element.142, f32[2]{0:T(128)S(1)} %get-tuple-element.143, ...), kind=kOutput, calls=%fused_computation.6.clone.1 | convolution fusion | flops 137954816 | bytes 1054736 | tf_op jit(solution)/shard_map/while/body/eval_jaxpr/hqk,khd->qhd/dot_general | solution.py:81
  243.2 19.6 %all_to_all.61 = bf16[8,512,128]{1,2,0:T(8,128)(2,1)S(1)} all-to-all(bf16[8,512,128]{1,2,0:T(8,128)(2,1)} %bitcast.134), channel_id=1, replica_groups=mesh['dp'=16,'mp'=8] {'mp'}, dimensions={0} | all-to-all | bytes 2097152 | tf_op jit(solution)/shard_map/all_to_all | solution.py:133
  262.7 2.3 fusion.49
  265.1 12.0 %convolution_bitcast_fusion = f32[2,512,2816]{2,1,0:T(8,128)} fusion(bf16[2,1024,2816]{2,1,0:T(8,128)(2,1)} %all-gather.6.cloned.1.call-done, bf16[512,1024]{1,0:T(8,128)(2,1)} %get-tuple-element.86, f32[1024]{0:T(1024)S(1)} %bitcast.141, f32[512]{0:T(512)S(1)} %add_rsqrt_fusion), kind=kOutput, calls=%fused_computation.32 | convolution fusion | flops 5907677184 | bytes 24123392 | tf_op jit(solution)/shard_map/rc,jcf->jrf/dot_general | solution.py:140
  277.1 10.1 %fusion.52 = bf16[512,1024]{1,0:T(8,128)(2,1)} fusion(bf16[512,1024]{1,0:T(8,128)(2,1)S(1)} %copy-done.3, bf16[2816,1024]{0,1:T(8,128)(2,1)} %all-gather.8.cloned.1.call-done, f32[2,512,2816]{2,1,0:T(8,128)} %convolution_bitcast_fusion), kind=kOutput, calls=%fused_computation.53 | convolution fusion | flops 2963013632 | bytes 19398656 | tf_op jit(solution)/shard_map/dot_general | solution.py:148
  (108 shorter events, 33.1 us)
Async XLA Ops:
  6.5 175.3 %copy-start = (f32[2,16]{1,0:T(2,128)S(1)}, f32[2,16]{1,0:T(2,128)}, u32[]{:S(2)}) copy-start(f32[2,16]{1,0:T(2,128)} %param.16) | copy-start | bytes 388
  6.5 15.8 %copy-start.8 = (bf16[2,64,352]{2,1,0:T(8,128)(2,1)S(1)}, bf16[2,64,352]{2,1,0:T(8,128)(2,1)}, u32[]{:S(2)}) copy-start(bf16[2,64,352]{2,1,0:T(8,128)(2,1)} %param.17) | copy-start | bytes 270340
  6.5 76.6 %all-gather.4.cloned.1.call-start = ((), (), s32[]{:S(2)}) async-start(), calls=%async_computation.7 | async-start | bytes 6684672 | tf_op jit(solution)/shard_map/all_gather | solution.py:120
  22.3 242.8 %all-gather.6.cloned.1.call-start = ((), (), s32[]{:S(2)}) async-start(), calls=%async_computation.8 | async-start | bytes 12255232 | tf_op jit(solution)/shard_map/all_gather | solution.py:143
  38.1 2.1 copy-start.10
  38.1 6.1 %copy-start.12 = (s32[512]{0:T(512)S(1)}, s32[512]{0:T(512)}, u32[]{:S(2)}) copy-start(s32[512]{0:T(512)} %param.21) | copy-start | bytes 6148
  38.1 6.2 %copy-start.4 = (bf16[512,1024]{1,0:T(8,128)(2,1)S(1)}, bf16[512,1024]{1,0:T(8,128)(2,1)}, u32[]{:S(2)}) copy-start(bf16[512,1024]{1,0:T(8,128)(2,1)} %param.12) | copy-start | bytes 3145732
  38.5 6.0 %copy-start.11 = (f32[2,1024]{1,0:T(2,128)S(1)}, f32[2,1024]{1,0:T(2,128)}, u32[]{:S(2)}) copy-start(f32[2,1024]{1,0:T(2,128)} %param.13) | copy-start | bytes 24580
  40.8 63.0 %all-to-all-start.3 = ((bf16[8,128,64]{1,2,0:T(8,128)(2,1)}), bf16[8,128,64]{1,2,0:T(8,128)(2,1)S(1)}, u32[]{:S(2)}, u32[]{:S(2)}) async-start(bf16[8,128,64]{1,2,0:T(8,128)(2,1)} %broadcast_in_dim.82), calls=%async_computation.3 | async-start | bytes 262144 | tf_op jit(solution)/shard_map/all_to_all | solution.py:12
  88.9 3.8 %copy-start.2 = (f32[3,512,1024]{2,1,0:T(8,128)}, f32[3,512,1024]{2,1,0:T(8,128)S(1)}, u32[]{:S(2)}) copy-start(f32[3,512,1024]{2,1,0:T(8,128)S(1)} %convolution_bitcast_fusion.1) | copy-start | bytes 18874372
  101.0 2.8 copy-start.9
  103.8 0.8 copy-start.6
  104.6 16.6 %all-to-all-start.6 = ((bf16[8,352,64]{1,2,0:T(8,128)(2,1)}), bf16[8,352,64]{1,2,0:T(8,128)(2,1)S(1)}, u32[]{:S(2)}, u32[]{:S(2)}) async-start(bf16[8,352,64]{1,2,0:T(8,128)(2,1)} %broadcast_in_dim.85), calls=%async_computation.6 | async-start | bytes 786432 | tf_op jit(solution)/shard_map/all_to_all | solution.py:12
  121.2 5.0 %copy-start.13 = (s32[512]{0:T(512)S(1)}, s32[512]{0:T(512)}, u32[]{:S(2)}) copy-start(s32[512]{0:T(512)} %param.20) | copy-start | bytes 6148
  121.2 5.0 %copy-start.14 = (s32[512]{0:T(512)S(1)}, s32[512]{0:T(512)}, u32[]{:S(2)}) copy-start(s32[512]{0:T(512)} %param.19) | copy-start | bytes 6148
  121.2 60.8 %copy-start.7 = (bf16[8,128,64]{1,2,0:T(8,128)(2,1)S(1)}, bf16[8,128,64]{1,2,0:T(8,128)(2,1)}, u32[]{:S(2)}) copy-start(bf16[8,128,64]{1,2,0:T(8,128)(2,1)} %copy-done.6) | copy-start | bytes 393220
  121.2 62.1 %all-to-all-start.1 = ((bf16[3,512,1024]{1,0,2:T(4,128)(2,1)}), bf16[3,512,1024]{1,0,2:T(4,128)(2,1)}, u32[]{:S(2)}, u32[]{:S(2)}) async-start(bf16[3,512,1024]{1,0,2:T(4,128)(2,1)} %copy.40), calls=%async_computation.1 | async-start | bytes 8388608 | tf_op jit(solution)/shard_map/all_to_all | solution.py:126
  126.1 151.0 %all-gather.8.cloned.1.call-start = ((), (), s32[]{:S(2)}) async-start(), calls=%async_computation.9 | async-start | bytes 6127616 | tf_op jit(solution)/shard_map/all_gather | solution.py:150
  184.9 58.3 %all-to-all-start.4 = ((bf16[16,1024,64]{1,2,0:T(8,128)(2,1)}), bf16[16,1024,64]{1,2,0:T(8,128)(2,1)S(1)}, u32[]{:S(2)}, u32[]{:S(2)}) async-start(bf16[16,1024,64]{1,2,0:T(8,128)(2,1)} %broadcast_in_dim.83), calls=%async_computation.4 | async-start | bytes 4194304 | tf_op jit(solution)/shard_map/all_to_all | solution.py:12
  243.2 19.6 %copy-start.5 = (bf16[512,1024]{1,0:T(8,128)(2,1)S(1)}, bf16[512,1024]{1,0:T(8,128)(2,1)}, u32[]{:S(2)}) copy-start(bf16[512,1024]{1,0:T(8,128)(2,1)} %param.12) | copy-start | bytes 3145732
  265.1 12.0 %copy-start.3 = (bf16[512,1024]{1,0:T(8,128)(2,1)S(1)}, bf16[512,1024]{1,0:T(8,128)(2,1)}, u32[]{:S(2)}) copy-start(bf16[512,1024]{1,0:T(8,128)(2,1)} %get-tuple-element.86) | copy-start | bytes 3145732
  277.1 10.1 %copy-start.1 = (f32[2,16]{1,0:T(2,128)S(1)}, f32[2,16]{1,0:T(2,128)}, u32[]{:S(2)}) copy-start(f32[2,16]{1,0:T(2,128)} %param.16) | copy-start | bytes 388
Sparse Core Ops, SparseCore 0:
  22.4 60.6 all-gather.3
  85.3 84.4 all-gather.5
  183.4 74.9 all-gather.7
where the time goes:
time: 295 us; the launch traced here: 294 us
  blocking collectives  105 us (36%)
  matrix products  73.9 us (25%)
  waiting for transfers between devices  38.4 us (13%)
  local copies, waits for them, and re-layouts  33.5 us (11%)
  starting transfers between devices  18.6 us (6%)
  between operations  13.4 us (5%)
  other arithmetic  11.1 us (4%)
    all_gather x1, blocking collectives, rows_first(): whole = lax.all_gather(both, axis, axis=0, tiled=True)  55.5 us
    all_gather x1, waiting for transfers between devices, local(): lax.all_gather(wide_columns, 'dp', axis=1, tiled=True)  38.3 us
    all_to_all x2, blocking collectives, sent_to_all(): return lax.all_to_all(copies, axis, split_axis=0, concat_axis=0, tiled=True)  29.6 us
    dot_general x8, matrix products, one_sequence(): jnp.einsum('hqk,khd->qhd', weights, vs, preferred_element_type=jnp.float32)  25.7 us
    all_to_all x1, blocking collectives, local(): lax.all_to_all(attended, 'mp', split_axis=0, concat_axis=1, tiled=True)  19.6 us
    sub x8, matrix products, one_sequence(): expo = jnp.exp(scores - top)  18 us
    all_to_all x3, starting transfers between devices, sent_to_all(): return lax.all_to_all(copies, axis, split_axis=0, concat_axis=0, tiled=True)  13.6 us
    dot_general x1, matrix products, local(): jnp.einsum('rc,jcf->jrf', columns, lax.all_gather(ffn_columns, 'dp', axis...  12 us
  transfers between devices with their start and end apart: 7, of which 1 were waited for; matrix products, arithmetic and copies ran while one was open for 36% of the time, Pallas kernels for 0%

commit v1 on v0

--- a/solution.py
+++ b/solution.py
@@ -114,10 +114,15 @@
     first_normed = rms_norm(tokens, norm_gain[0])
     wide_columns = collect(qkv_weight, "mp", 2)
     columns = first_normed
+
+    def _supply_indices(my_data, group_axis):
+        passed = lax.all_gather(my_data, group_axis)
+        return jnp.concatenate(passed, 1)
+
     projected = jnp.einsum(
         "rc,jcd->jrd",
         columns,
-        lax.all_gather(wide_columns, "dp", axis=1, tiled=True),
+        _supply_indices(wide_columns, "dp"),
         preferred_element_type=jnp.float32,
     )
     queries = rotated(projected[0], time_ids)

time: 295 us -> 297 us (level)
  local copies, waits for them, and re-layouts: 33.5 us -> 37.5 us
    reshape x0 -> x1, local copies, waits for them, and re-layouts: none -> 3.49 us  [_supply_indices(): return jnp.concatenate(passed, 1)]
where the time goes in v1:
time: 297 us; the launch traced here: 295 us
  blocking collectives  105 us (35%)
  matrix products  71.7 us (24%)
  waiting for transfers between devices  38.4 us (13%)
  local copies, waits for them, and re-layouts  37.5 us (13%)
  starting transfers between devices  18.4 us (6%)
  between operations  13.4 us (5%)
  other arithmetic  11.1 us (4%)
    all_gather x1, blocking collectives, rows_first(): whole = lax.all_gather(both, axis, axis=0, tiled=True)  55.5 us
    all_gather x1, waiting for transfers between devices, _supply_indices(): passed = lax.all_gather(my_data, group_axis)  38.3 us
    all_to_all x2, blocking collectives, sent_to_all(): return lax.all_to_all(copies, axis, split_axis=0, concat_axis=0, tiled=True)  29.6 us
    dot_general x8, matrix products, one_sequence(): jnp.einsum('hqk,khd->qhd', weights, vs, preferred_element_type=jnp.float32)  25.7 us
    all_to_all x1, blocking collectives, local(): lax.all_to_all(attended, 'mp', split_axis=0, concat_axis=1, tiled=True)  19.6 us
    sub x8, matrix products, one_sequence(): expo = jnp.exp(scores - top)  18 us
    all_to_all x3, starting transfers between devices, sent_to_all(): return lax.all_to_all(copies, axis, split_axis=0, concat_axis=0, tiled=True)  13.4 us
    dot_general x1, matrix products, local(): jnp.einsum('rc,jcf->jrf', columns, lax.all_gather(ffn_columns, 'dp', axis...  12 us
  transfers between devices with their start and end apart: 7, of which 1 were waited for; matrix products, arithmetic and copies ran while one was open for 36% of the time, Pallas kernels for 0%

profile of v1, /device:TPU:2, one launch (start us, length us, event | category | flops | bytes accessed | tf_op | source)
XLA Modules:
  0.0 295.4 jit_solution(8293301190600336016)
XLA Ops:
  7.5 14.0 %all_to_all.59 = bf16[8,3,64,128]{3,2,1,0:T(8,128)(2,1)S(1)} all-to-all(bf16[8,3,64,128]{3,2,1,0:T(8,128)(2,1)S(1)} %broadcast_in_dim.81), channel_id=1, replica_groups=mesh['dp'=16,'mp'=8] {'mp'}, dimensions={0} | all-to-all | bytes 786432 | tf_op jit(solution)/shard_map/all_to_all | solution.py:12
  22.8 15.6 %all_to_all.60 = bf16[8,2,64,352]{3,2,1,0:T(8,128)(2,1)S(1)} all-to-all(bf16[8,2,64,352]{3,2,1,0:T(8,128)(2,1)S(1)} %broadcast_in_dim.84), channel_id=1, replica_groups=mesh['dp'=16,'mp'=8] {'mp'}, dimensions={0} | all-to-all | bytes 1441792 | tf_op jit(solution)/shard_map/all_to_all | solution.py:12
  41.2 3.4 %all-to-all-start.3 = ((bf16[8,128,64]{1,2,0:T(8,128)(2,1)}), bf16[8,128,64]{1,2,0:T(8,128)(2,1)S(1)}, u32[]{:S(2)}, u32[]{:S(2)}) async-start(bf16[8,128,64]{1,2,0:T(8,128)(2,1)} %broadcast_in_dim.82), calls=%async_computation.3 | async-start | bytes 262144 | tf_op jit(solution)/shard_map/all_to_all | solution.py:12
  45.2 38.3 %all-gather.4.cloned.1.call-done = bf16[16,3,64,1024]{3,2,1,0:T(8,128)(2,1)} async-done(((bf16[1,3,64,1024]{3,2,1,0:T(8,128)(2,1)}), bf16[16,3,64,1024]{3,2,1,0:T(8,128)(2,1)}) %all-gather.4.cloned.1.call-update) | async-done | bytes 6291472 | tf_op jit(solution)/shard_map/all_gather | solution.py:119
  83.5 3.5 %copy.47 = bf16[3,16,64,1024]{3,2,1,0:T(8,128)(2,1)S(1)} copy(bf16[3,16,64,1024]{3,2,0,1:T(8,128)(2,1)} %bitcast.129) | data formatting | bytes 12582912 | tf_op jit(solution)/shard_map/reshape | solution.py:120
  87.0 3.6 %convolution_bitcast_fusion.1 = f32[3,512,1024]{2,1,0:T(8,128)S(1)} fusion(bf16[3,1024,1024]{2,1,0:T(8,128)(2,1)S(1)} %bitcast.130, bf16[512,1024]{1,0:T(8,128)(2,1)S(1)} %copy-done.4, f32[1024]{0:T(1024)S(1)} %bitcast.144, f32[512]{0:T(512)S(1)} %add_rsqrt_fusion.1), kind=kOutput, calls=%fused_computation.45 | convolution fusion | flops 3223322624 | bytes 13637632 | tf_op jit(solution)/shard_map/rc,jcd->jrd/dot_general | solution.py:122
  90.6 2.5 fusion.69
  96.6 3.0 %copy.49 = f32[1,512,1024]{1,2,0:T(8,128)} copy(f32[1,512,1024]{2,1,0:T(8,128)} %get-tuple-element.71) | data formatting | bytes 4194304 | tf_op jit(solution)/shard_map/slice | solution.py:129
  99.6 3.3 %subtract_convert_fusion.1 = (bf16[512,16,32]{0,2,1:T(8,128)(2,1)S(1)}, bf16[512,16,32]{0,2,1:T(8,128)(2,1)S(1)}, bf16[512,16,32]{0,2,1:T(8,128)(2,1)}, bf16[512,16,32]{0,2,1:T(8,128)(2,1)}) fusion(f32[512,16,64]{0,2,1:T(8,128)S(1)} %bitcast.127, f32[512,32]{0,1:T(8,128)S(1)} %get-tuple-element.84, f32[512,32]{0,1:T(8,128)S(1)} %get-tuple-element.83, ...), kind=kLoop, calls=%fused_computation.64 | loop fusion | flops 4194304 | bytes 6422528 | tf_op jit(solution)/shard_map/convert.3
  102.9 2.8 slice.103
  106.4 4.4 %all-to-all-start.6 = ((bf16[8,352,64]{1,2,0:T(8,128)(2,1)}), bf16[8,352,64]{1,2,0:T(8,128)(2,1)S(1)}, u32[]{:S(2)}, u32[]{:S(2)}) async-start(bf16[8,352,64]{1,2,0:T(8,128)(2,1)} %broadcast_in_dim.85), calls=%async_computation.6 | async-start | bytes 786432 | tf_op jit(solution)/shard_map/all_to_all | solution.py:12
  117.3 5.7 %copy.52 = bf16[3,512,1024]{1,0,2:T(4,128)(2,1)} copy(bf16[3,512,1024]{2,1,0:T(8,128)(2,1)S(1)} %pad_maximum_fusion) | data formatting | bytes 6291456 | tf_op jit(solution)/shard_map/stack | solution.py:132
  123.0 4.9 %all-to-all-start.1 = ((bf16[3,512,1024]{1,0,2:T(4,128)(2,1)}), bf16[3,512,1024]{1,0,2:T(4,128)(2,1)}, u32[]{:S(2)}, u32[]{:S(2)}) async-start(bf16[3,512,1024]{1,0,2:T(4,128)(2,1)} %copy.52), calls=%async_computation.1 | async-start | bytes 8388608 | tf_op jit(solution)/shard_map/all_to_all | solution.py:131
  128.1 55.5 %all_gather.13 = s32[4096,2]{0,1:T(2,128)S(1)} all-gather(s32[512,2]{0,1:T(2,128)S(1)} %pad_add_fusion), channel_id=1, replica_groups=mesh['dp'=16,'mp'=8] {'mp'}, dimensions={0}, use_global_device_ids=true | all-gather | bytes 36864 | tf_op jit(solution)/shard_map/all_gather | solution.py:30
  186.7 5.6 %all-to-all-start.4 = ((bf16[16,1024,64]{1,2,0:T(8,128)(2,1)}), bf16[16,1024,64]{1,2,0:T(8,128)(2,1)S(1)}, u32[]{:S(2)}, u32[]{:S(2)}) async-start(bf16[16,1024,64]{1,2,0:T(8,128)(2,1)} %broadcast_in_dim.83), calls=%async_computation.4 | async-start | bytes 4194304 | tf_op jit(solution)/shard_map/all_to_all | solution.py:12
  192.3 3.2 %copy.53 = bf16[3,512,1024]{1,2,0:T(8,128)(2,1)S(1)} copy(bf16[3,512,1024]{1,0,2:T(4,128)(2,1)} %all-to-all-done.1) | data formatting | bytes 6291456 | tf_op jit(solution)/shard_map/all_to_all | solution.py:131
  197.3 47.4 %while.10 = (s32[]{:T(128)}, bf16[8,512,2,64]{1,3,2,0:T(8,128)(2,1)}, bf16[8,512,2,64]{1,3,2,0:T(8,128)(2,1)}, s32[8,512]{1,0:T(8,128)S(1)}, bf16[8,512,2,64]{1,...) while((s32[]{:T(128)}, ...), condition=%wide.region_4.5_spmd, body=%wide.region_1.4_spmd.sunk | while | flops 208734208 | bytes 2383009 | solution.py:86
  200.0 3.2 %fusion.91 = bf16[8,512,2,64]{1,3,2,0:T(8,128)(2,1)} fusion(bf16[8,512,2,64]{1,3,2,0:T(8,128)(2,1)} %get-tuple-element.156, s32[]{:T(128)} %get-tuple-element.155, f32[2,512]{1,0:T(2,128)S(1)} %fusion.90, bf16[8,512,2,64]{1,3,2,0:T(8,128)(2,1)} %get-tuple-element.166, f32[2]{0:T(128)S(1)} %get-tuple-element.142, f32[2]{0:T(128)S(1)} %get-tuple-element.143, ...), kind=kOutput, calls=%fused_computation.6.clone.1 | convolution fusion | flops 137954816 | bytes 1054736 | tf_op jit(solution)/shard_map/while/body/eval_jaxpr/hqk,khd->qhd/dot_general | solution.py:81
  203.7 2.2 fusion.90
  205.9 3.2 %fusion.91 = bf16[8,512,2,64]{1,3,2,0:T(8,128)(2,1)} fusion(bf16[8,512,2,64]{1,3,2,0:T(8,128)(2,1)} %get-tuple-element.156, s32[]{:T(128)} %get-tuple-element.155, f32[2,512]{1,0:T(2,128)S(1)} %fusion.90, bf16[8,512,2,64]{1,3,2,0:T(8,128)(2,1)} %get-tuple-element.166, f32[2]{0:T(128)S(1)} %get-tuple-element.142, f32[2]{0:T(128)S(1)} %get-tuple-element.143, ...), kind=kOutput, calls=%fused_computation.6.clone.1 | convolution fusion | flops 137954816 | bytes 1054736 | tf_op jit(solution)/shard_map/while/body/eval_jaxpr/hqk,khd->qhd/dot_general | solution.py:81
  211.8 3.2 %fusion.91 = bf16[8,512,2,64]{1,3,2,0:T(8,128)(2,1)} fusion(bf16[8,512,2,64]{1,3,2,0:T(8,128)(2,1)} %get-tuple-element.156, s32[]{:T(128)} %get-tuple-element.155, f32[2,512]{1,0:T(2,128)S(1)} %fusion.90, bf16[8,512,2,64]{1,3,2,0:T(8,128)(2,1)} %get-tuple-element.166, f32[2]{0:T(128)S(1)} %get-tuple-element.142, f32[2]{0:T(128)S(1)} %get-tuple-element.143, ...), kind=kOutput, calls=%fused_computation.6.clone.1 | convolution fusion | flops 137954816 | bytes 1054736 | tf_op jit(solution)/shard_map/while/body/eval_jaxpr/hqk,khd->qhd/dot_general | solution.py:81
  217.7 3.2 %fusion.91 = bf16[8,512,2,64]{1,3,2,0:T(8,128)(2,1)} fusion(bf16[8,512,2,64]{1,3,2,0:T(8,128)(2,1)} %get-tuple-element.156, s32[]{:T(128)} %get-tuple-element.155, f32[2,512]{1,0:T(2,128)S(1)} %fusion.90, bf16[8,512,2,64]{1,3,2,0:T(8,128)(2,1)} %get-tuple-element.166, f32[2]{0:T(128)S(1)} %get-tuple-element.142, f32[2]{0:T(128)S(1)} %get-tuple-element.143, ...), kind=kOutput, calls=%fused_computation.6.clone.1 | convolution fusion | flops 137954816 | bytes 1054736 | tf_op jit(solution)/shard_map/while/body/eval_jaxpr/hqk,khd->qhd/dot_general | solution.py:81
  223.6 3.2 %fusion.91 = bf16[8,512,2,64]{1,3,2,0:T(8,128)(2,1)} fusion(bf16[8,512,2,64]{1,3,2,0:T(8,128)(2,1)} %get-tuple-element.156, s32[]{:T(128)} %get-tuple-element.155, f32[2,512]{1,0:T(2,128)S(1)} %fusion.90, bf16[8,512,2,64]{1,3,2,0:T(8,128)(2,1)} %get-tuple-element.166, f32[2]{0:T(128)S(1)} %get-tuple-element.142, f32[2]{0:T(128)S(1)} %get-tuple-element.143, ...), kind=kOutput, calls=%fused_computation.6.clone.1 | convolution fusion | flops 137954816 | bytes 1054736 | tf_op jit(solution)/shard_map/while/body/eval_jaxpr/hqk,khd->qhd/dot_general | solution.py:81
  229.6 3.2 %fusion.91 = bf16[8,512,2,64]{1,3,2,0:T(8,128)(2,1)} fusion(bf16[8,512,2,64]{1,3,2,0:T(8,128)(2,1)} %get-tuple-element.156, s32[]{:T(128)} %get-tuple-element.155, f32[2,512]{1,0:T(2,128)S(1)} %fusion.90, bf16[8,512,2,64]{1,3,2,0:T(8,128)(2,1)} %get-tuple-element.166, f32[2]{0:T(128)S(1)} %get-tuple-element.142, f32[2]{0:T(128)S(1)} %get-tuple-element.143, ...), kind=kOutput, calls=%fused_computation.6.clone.1 | convolution fusion | flops 137954816 | bytes 1054736 | tf_op jit(solution)/shard_map/while/body/eval_jaxpr/hqk,khd->qhd/dot_general | solution.py:81
  233.2 2.4 fusion.90
  235.6 3.2 %fusion.91 = bf16[8,512,2,64]{1,3,2,0:T(8,128)(2,1)} fusion(bf16[8,512,2,64]{1,3,2,0:T(8,128)(2,1)} %get-tuple-element.156, s32[]{:T(128)} %get-tuple-element.155, f32[2,512]{1,0:T(2,128)S(1)} %fusion.90, bf16[8,512,2,64]{1,3,2,0:T(8,128)(2,1)} %get-tuple-element.166, f32[2]{0:T(128)S(1)} %get-tuple-element.142, f32[2]{0:T(128)S(1)} %get-tuple-element.143, ...), kind=kOutput, calls=%fused_computation.6.clone.1 | convolution fusion | flops 137954816 | bytes 1054736 | tf_op jit(solution)/shard_map/while/body/eval_jaxpr/hqk,khd->qhd/dot_general | solution.py:81
  239.3 2.2 fusion.90
  241.5 3.2 %fusion.91 = bf16[8,512,2,64]{1,3,2,0:T(8,128)(2,1)} fusion(bf16[8,512,2,64]{1,3,2,0:T(8,128)(2,1)} %get-tuple-element.156, s32[]{:T(128)} %get-tuple-element.155, f32[2,512]{1,0:T(2,128)S(1)} %fusion.90, bf16[8,512,2,64]{1,3,2,0:T(8,128)(2,1)} %get-tuple-element.166, f32[2]{0:T(128)S(1)} %get-tuple-element.142, f32[2]{0:T(128)S(1)} %get-tuple-element.143, ...), kind=kOutput, calls=%fused_computation.6.clone.1 | convolution fusion | flops 137954816 | bytes 1054736 | tf_op jit(solution)/shard_map/while/body/eval_jaxpr/hqk,khd->qhd/dot_general | solution.py:81
  244.8 19.6 %all_to_all.61 = bf16[8,512,128]{1,2,0:T(8,128)(2,1)S(1)} all-to-all(bf16[8,512,128]{1,2,0:T(8,128)(2,1)} %bitcast.136), channel_id=1, replica_groups=mesh['dp'=16,'mp'=8] {'mp'}, dimensions={0} | all-to-all | bytes 2097152 | tf_op jit(solution)/shard_map/all_to_all | solution.py:138
  264.3 2.3 fusion.49
  266.7 12.0 %convolution_bitcast_fusion = f32[2,512,2816]{2,1,0:T(8,128)} fusion(bf16[2,1024,2816]{2,1,0:T(8,128)(2,1)} %all-gather.6.cloned.1.call-done, bf16[512,1024]{1,0:T(8,128)(2,1)} %get-tuple-element.86, f32[1024]{0:T(1024)S(1)} %bitcast.143, f32[512]{0:T(512)S(1)} %add_rsqrt_fusion), kind=kOutput, calls=%fused_computation.32 | convolution fusion | flops 5907677184 | bytes 24123392 | tf_op jit(solution)/shard_map/rc,jcf->jrf/dot_general | solution.py:145
  278.7 10.1 %fusion.52 = bf16[512,1024]{1,0:T(8,128)(2,1)} fusion(bf16[512,1024]{1,0:T(8,128)(2,1)S(1)} %copy-done.3, bf16[2816,1024]{0,1:T(8,128)(2,1)} %all-gather.8.cloned.1.call-done, f32[2,512,2816]{2,1,0:T(8,128)} %convolution_bitcast_fusion), kind=kOutput, calls=%fused_computation.53 | convolution fusion | flops 2963013632 | bytes 19398656 | tf_op jit(solution)/shard_map/dot_general | solution.py:153
  (110 shorter events, 35.9 us)
Async XLA Ops:
  6.5 177.2 %copy-start = (f32[2,16]{1,0:T(2,128)S(1)}, f32[2,16]{1,0:T(2,128)}, u32[]{:S(2)}) copy-start(f32[2,16]{1,0:T(2,128)} %param.16) | copy-start | bytes 388
  6.5 16.2 %copy-start.8 = (bf16[2,64,352]{2,1,0:T(8,128)(2,1)S(1)}, bf16[2,64,352]{2,1,0:T(8,128)(2,1)}, u32[]{:S(2)}) copy-start(bf16[2,64,352]{2,1,0:T(8,128)(2,1)} %param.17) | copy-start | bytes 270340
  6.5 77.0 %all-gather.4.cloned.1.call-start = ((), (), s32[]{:S(2)}) async-start(), calls=%async_computation.7 | async-start | bytes 6684672 | tf_op jit(solution)/shard_map/all_gather | solution.py:119
  22.7 244.0 %all-gather.6.cloned.1.call-start = ((), (), s32[]{:S(2)}) async-start(), calls=%async_computation.8 | async-start | bytes 12255232 | tf_op jit(solution)/shard_map/all_gather | solution.py:148
  38.4 2.1 copy-start.10
  38.4 6.1 %copy-start.12 = (s32[512]{0:T(512)S(1)}, s32[512]{0:T(512)}, u32[]{:S(2)}) copy-start(s32[512]{0:T(512)} %param.21) | copy-start | bytes 6148
  38.4 6.2 %copy-start.4 = (bf16[512,1024]{1,0:T(8,128)(2,1)S(1)}, bf16[512,1024]{1,0:T(8,128)(2,1)}, u32[]{:S(2)}) copy-start(bf16[512,1024]{1,0:T(8,128)(2,1)} %param.12) | copy-start | bytes 3145732
  38.9 6.0 %copy-start.11 = (f32[2,1024]{1,0:T(2,128)S(1)}, f32[2,1024]{1,0:T(2,128)}, u32[]{:S(2)}) copy-start(f32[2,1024]{1,0:T(2,128)} %param.13) | copy-start | bytes 24580
  41.2 64.5 %all-to-all-start.3 = ((bf16[8,128,64]{1,2,0:T(8,128)(2,1)}), bf16[8,128,64]{1,2,0:T(8,128)(2,1)S(1)}, u32[]{:S(2)}, u32[]{:S(2)}) async-start(bf16[8,128,64]{1,2,0:T(8,128)(2,1)} %broadcast_in_dim.82), calls=%async_computation.3 | async-start | bytes 262144 | tf_op jit(solution)/shard_map/all_to_all | solution.py:12
  90.6 3.9 %copy-start.2 = (f32[3,512,1024]{2,1,0:T(8,128)}, f32[3,512,1024]{2,1,0:T(8,128)S(1)}, u32[]{:S(2)}) copy-start(f32[3,512,1024]{2,1,0:T(8,128)S(1)} %convolution_bitcast_fusion.1) | copy-start | bytes 18874372
  102.9 2.8 copy-start.9
  105.6 0.8 copy-start.6
  106.4 16.6 %all-to-all-start.6 = ((bf16[8,352,64]{1,2,0:T(8,128)(2,1)}), bf16[8,352,64]{1,2,0:T(8,128)(2,1)S(1)}, u32[]{:S(2)}, u32[]{:S(2)}) async-start(bf16[8,352,64]{1,2,0:T(8,128)(2,1)} %broadcast_in_dim.85), calls=%async_computation.6 | async-start | bytes 786432 | tf_op jit(solution)/shard_map/all_to_all | solution.py:12
  123.0 5.0 %copy-start.13 = (s32[512]{0:T(512)S(1)}, s32[512]{0:T(512)}, u32[]{:S(2)}) copy-start(s32[512]{0:T(512)} %param.20) | copy-start | bytes 6148
  123.0 5.0 %copy-start.14 = (s32[512]{0:T(512)S(1)}, s32[512]{0:T(512)}, u32[]{:S(2)}) copy-start(s32[512]{0:T(512)} %param.19) | copy-start | bytes 6148
  123.0 60.8 %copy-start.7 = (bf16[8,128,64]{1,2,0:T(8,128)(2,1)S(1)}, bf16[8,128,64]{1,2,0:T(8,128)(2,1)}, u32[]{:S(2)}) copy-start(bf16[8,128,64]{1,2,0:T(8,128)(2,1)} %copy-done.6) | copy-start | bytes 393220
  123.0 62.1 %all-to-all-start.1 = ((bf16[3,512,1024]{1,0,2:T(4,128)(2,1)}), bf16[3,512,1024]{1,0,2:T(4,128)(2,1)}, u32[]{:S(2)}, u32[]{:S(2)}) async-start(bf16[3,512,1024]{1,0,2:T(4,128)(2,1)} %copy.52), calls=%async_computation.1 | async-start | bytes 8388608 | tf_op jit(solution)/shard_map/all_to_all | solution.py:131
  128.0 150.7 %all-gather.8.cloned.1.call-start = ((), (), s32[]{:S(2)}) async-start(), calls=%async_computation.9 | async-start | bytes 6127616 | tf_op jit(solution)/shard_map/all_gather | solution.py:155
  186.7 58.0 %all-to-all-start.4 = ((bf16[16,1024,64]{1,2,0:T(8,128)(2,1)}), bf16[16,1024,64]{1,2,0:T(8,128)(2,1)S(1)}, u32[]{:S(2)}, u32[]{:S(2)}) async-start(bf16[16,1024,64]{1,2,0:T(8,128)(2,1)} %broadcast_in_dim.83), calls=%async_computation.4 | async-start | bytes 4194304 | tf_op jit(solution)/shard_map/all_to_all | solution.py:12
  244.8 19.6 %copy-start.5 = (bf16[512,1024]{1,0:T(8,128)(2,1)S(1)}, bf16[512,1024]{1,0:T(8,128)(2,1)}, u32[]{:S(2)}) copy-start(bf16[512,1024]{1,0:T(8,128)(2,1)} %param.12) | copy-start | bytes 3145732
  266.7 12.0 %copy-start.3 = (bf16[512,1024]{1,0:T(8,128)(2,1)S(1)}, bf16[512,1024]{1,0:T(8,128)(2,1)}, u32[]{:S(2)}) copy-start(bf16[512,1024]{1,0:T(8,128)(2,1)} %get-tuple-element.86) | copy-start | bytes 3145732
  278.7 10.1 %copy-start.1 = (f32[2,16]{1,0:T(2,128)S(1)}, f32[2,16]{1,0:T(2,128)}, u32[]{:S(2)}) copy-start(f32[2,16]{1,0:T(2,128)} %param.16) | copy-start | bytes 388
Sparse Core Ops, SparseCore 0:
  22.8 60.6 all-gather.3
  85.6 84.4 all-gather.5
  185.3 74.6 all-gather.7
